TPU v7x, 32 devices: a whole 2x2x4 slice. The times are simulated.
32 devices in a mesh: pb: 4 (over z), freq: 4 (over y, core), ga: 2 (over x).
Axes of the slice: x: 2, y: 2, z: 4, core: 2. Of those that a mesh axis runs over, the one named last changes fastest.
Arguments:
- densities: bfloat16 [4, 2, 256, 4096], P('pb', None, ('freq', 'ga')), may hold values from -0.5 to 0.5
- screened: bfloat16 [4, 4, 2, 4096, 4096], P('pb', 'freq', None, 'ga'), may hold values from -0.09375 to 0.09375
- energies: float32 [16, 256], replicated, may hold values from -2.5 to 2.5
- occupied: int32 [16], replicated, may hold values from 64 to 192
- kmq: int32 [4], replicated, may hold values from 0 to 15
- offsets: int32 [4], replicated, may hold values from -16 to 15
- weights: float32 [4], replicated, may hold values from 0.5 to 2
Outputs:
- sigma: float32 [2, 1, 64], P(None, None, ('pb', 'freq'))
All inputs are finite; a program needn't handle non-finite values.
Results may differ from a plain program's by a relative error of at most 0.0003.
Values may be sent and summed in bfloat16 or wider, within the bound.
A program may use at most 64 MiB of HBM per device.

v0:
```python
import math
import jax
import jax.numpy as jnp
from jax import lax
from jax.sharding import PartitionSpec as P

NB = 256
NS = 1
OUT_DEV = 4
broadening = 0.15


def from_behind(block, axis, distance):
    devices = range(lax.axis_size(axis))
    route = [((i - distance) % len(devices), i) for i in devices]
    return lax.ppermute(block, axis, route)


def green_parts(level_row, filled, freq_shift, omegas):
    bands = jnp.arange(level_row.shape[0], dtype=jnp.int32)
    pole_sign = jnp.where(bands < filled, -1.0, 1.0).astype(jnp.float32)
    real_part = omegas[None, :] - freq_shift - level_row[:, None]
    imag_part = broadening * pole_sign[:, None]
    denominator = real_part * real_part + imag_part * imag_part
    return (real_part / denominator, -imag_part / denominator)


def spectrum(pair_real, pair_imag, green_real, green_imag):
    exact = lax.Precision.HIGHEST
    real_out = jnp.dot(pair_real, green_real, precision=exact) - jnp.dot(
        pair_imag, green_imag, precision=exact
    )
    imag_out = jnp.dot(pair_real, green_imag, precision=exact) + jnp.dot(
        pair_imag, green_real, precision=exact
    )
    return jnp.stack([real_out, imag_out])


def panel_product(density_all, screen):
    pair_rows = density_all.shape[1]
    panel_rows = screen.shape[1]
    product = lax.dot_general(
        density_all.reshape(2 * pair_rows, -1),
        screen.reshape(2 * panel_rows, -1),
        (((1,), (1,)), ((), ())),
        preferred_element_type=jnp.float32,
    )
    product = product.reshape(2, pair_rows, 2, panel_rows)
    return (product[0, :, 0] - product[1, :, 1], product[0, :, 1] + product[1, :, 0])


def body(densities, screened, energies, occupied, kmq, offsets, weights):
    qpoint = lax.axis_index("pb")
    my_freq = lax.axis_index("freq")
    my_panel = lax.axis_index("ga")
    count_pb = lax.axis_size("pb")
    count_freq = lax.axis_size("freq")
    screen = screened[0, 0]
    panel_width = screen.shape[1]
    local_block = densities[0]
    whole = lax.all_gather(local_block, ("freq", "ga"), axis=1, tiled=True)
    real_x, imag_x = panel_product(whole, screen)
    own_rows = lax.dynamic_slice_in_dim(whole, my_panel * panel_width, panel_width, 2)
    dense = own_rows.astype(jnp.float32)
    real_sum = jnp.sum(dense[0] * real_x + dense[1] * imag_x, axis=1)
    imag_sum = jnp.sum(dense[0] * imag_x - dense[1] * real_x, axis=1)
    pair_total = lax.psum(jnp.stack([real_sum, imag_sum]), "ga")
    weighted = (pair_total * weights[my_freq]).reshape(2, NS, NB)
    kpoint = kmq[qpoint]
    level_row = energies[kpoint]
    filled = occupied[kpoint]
    total_out = OUT_DEV * count_pb * count_freq
    index_grid = (jnp.arange(count_pb, dtype=jnp.int32)[:, None] * count_freq + my_freq) * OUT_DEV
    index_grid = (index_grid + jnp.arange(OUT_DEV, dtype=jnp.int32)[None, :]).reshape(-1)
    omegas = -2.0 + 4.0 * index_grid.astype(jnp.float32) / total_out
    summed = jnp.zeros((2, NS, count_pb * OUT_DEV), jnp.float32)
    passed = weighted
    for rotation in range(count_freq):
        anchor = (my_freq - rotation) % count_freq
        freq_shift = 4.0 * offsets[anchor].astype(jnp.float32) / total_out
        green_real, green_imag = green_parts(level_row, filled, freq_shift, omegas)
        summed = summed + spectrum(passed[0], passed[1], green_real, green_imag)
        if rotation + 1 < count_freq:
            passed = from_behind(passed, "freq", 1)
    local_part = lax.psum_scatter(summed, "pb", scatter_dimension=2, tiled=True)
    prefactor = 1.0 / (2.0 * math.pi * count_pb)
    return jnp.stack([-prefactor * local_part[1], prefactor * local_part[0]])


def solution(mesh):
    placed = (
        P("pb", None, ("freq", "ga"), None),
        P("pb", "freq", None, "ga", None),
        P(),
        P(),
        P(),
        P(),
        P(),
    )
    return jax.shard_map(
        body, mesh=mesh, in_specs=placed, out_specs=P(None, None, ("pb", "freq")), check_vma=False
    )
```

profile of v0, /device:TPU:0, one launch (start us, length us, event | category | flops | bytes accessed | tf_op | source)
XLA Modules:
  0.0 112.7 jit_solution(8596917107336101058)
XLA Ops:
  6.5 0.7 all-gather.3.cloned.1.call-update
  7.3 1.2 %dynamic_slice.30 = s32[1]{0:T(128)} dynamic-slice(s32[4]{0:T(128)} %param.11, s32[]{:T(128)S(6)} %select_n.62), dynamic_slice_sizes={1} | dynamic-slice | bytes 12 | tf_op jit(solution)/shard_map/dynamic_slice | solution.py:69
  9.9 1.5 %fusion.102 = (s32[1]{0:T(128)}, s32[1]{0:T(128)}, s32[1]{0:T(128)}, s32[1]{0:T(128)}) fusion(s32[4]{0:T(128)} %param.12, s32[]{:T(128)S(6)} %select_n.70, s32[]{:T(128)S(6)} %select_n.66, s32[]{:T(128)S(6)} %select_n.61, s32[]{:T(128)S(6)} %select_n.68), kind=kLoop, calls=%fused_computation.143 | loop fusion | bytes 48 | tf_op jit(solution)/shard_map/dynamic_slice | solution.py:80
  14.2 1.3 %dynamic-slice.1 = u32[1]{0:T(128)} dynamic-slice(u32[32]{0:T(128)} %constant.95, u32[]{:T(128)S(6)} %add.222), dynamic_slice_sizes={1} | dynamic-slice | bytes 12
  16.1 1.3 %dynamic_slice.28 = f32[1]{0:T(128)} dynamic-slice(f32[4]{0:T(128)} %param.13, s32[]{:T(128)S(6)} %select_n.59), dynamic_slice_sizes={1} | dynamic-slice | bytes 12 | tf_op jit(solution)/shard_map/dynamic_slice | solution.py:68
  18.1 1.2 %dynamic_slice.32 = s32[1]{0:T(128)} dynamic-slice(s32[16]{0:T(128)} %param.10, s32[]{:T(128)S(6)} %select_n.63), dynamic_slice_sizes={1} | dynamic-slice | bytes 12 | tf_op jit(solution)/shard_map/dynamic_slice | solution.py:71
  19.3 0.7 fusion.100
  20.0 28.6 %all-gather.3.cloned.1.call-done = bf16[1,2,256,4096]{3,2,1,0:T(8,128)(2,1)} async-done(((bf16[1,2,32,4096]{3,2,1,0:T(8,128)(2,1)}), bf16[1,2,256,4096]{3,2,1,0:T(8,128)(2,1)}) %all-gather.3.cloned.1.call-update) | async-done | bytes 4194320 | tf_op jit(solution)/shard_map/all_gather | solution.py:61
  48.6 2.1 %dynamic-slice_convert_fusion = f32[1,2,256,2048]{3,2,1,0:T(8,128)S(1)} fusion(bf16[1,2,256,4096]{3,2,1,0:T(8,128)(2,1)} %all-gather.3.cloned.1.call-done, s32[]{:T(128)S(6)} %select_n.58), kind=kLoop, calls=%fused_computation.9 | loop fusion | flops 1048576 | bytes 6291460 | tf_op jit(solution)/shard_map/convert_element_type | solution.py:64
  50.7 22.8 %fusion = f32[2,256,2,2048]{3,1,2,0:T(8,128)S(1)} fusion(bf16[1,1,2,2048,4096]{4,3,2,1,0:T(8,128)(2,1)} %param.8, bf16[1,2,256,4096]{3,2,1,0:T(8,128)(2,1)} %all-gather.3.cloned.1.call-done), kind=kOutput, calls=%fused_computation | convolution fusion | flops 17179869184 | bytes 46137344 | tf_op jit(solution)/shard_map/dot_general | solution.py:42
  73.5 1.2 %add_reduce_fusion = (f32[256]{0:T(256)S(1)}, f32[256]{0:T(256)S(1)}) fusion(f32[1,2,256,2048]{3,2,1,0:T(8,128)S(1)} %dynamic-slice_convert_fusion, f32[2,256,2,2048]{3,1,2,0:T(8,128)S(1)} %fusion), kind=kLoop, calls=%fused_computation.11 | loop fusion | flops 5242368 | bytes 12584960 | tf_op jit(solution)/shard_map/reduce_sum | solution.py:65
  74.7 4.9 %psum.7 = f32[2,256]{1,0:T(2,128)S(1)} all-reduce(f32[2,256]{1,0:T(2,128)S(1)} %pad_maximum_fusion), channel_id=1, replica_groups=mesh['pb'=4,'freq'=4,'ga'=2] {'ga'}, use_global_device_ids=true, to_apply=%region_2.0 | all-reduce | flops 512 | bytes 4096 | tf_op jit(solution)/shard_map/psum | solution.py:67
  79.7 0.6 broadcast_multiply_fusion
  80.3 0.6 fusion.103
  80.9 0.3 convolution_bitcast_fusion.15
  81.2 0.3 convolution_bitcast_fusion.13
  81.5 0.3 fusion.13
  81.9 0.3 fusion.14
  82.2 2.7 %collective-permute-done = f32[2,1,256]{2,0,1:T(2,128)S(1)} collective-permute-done((f32[2,1,256]{2,0,1:T(2,128)S(1)}, f32[2,1,256]{2,0,1:T(2,128)S(1)}, u32[]{:S(2)}, u32[]{:S(2)}) %collective-permute-start) | collective-permute-done | bytes 2080 | tf_op jit(solution)/shard_map/ppermute | solution.py:16
  85.2 0.3 convolution_bitcast_fusion.10
  85.6 0.3 fusion.16
  85.9 0.3 fusion.15
  86.2 2.4 %collective-permute-done.1 = f32[2,1,256]{2,0,1:T(2,128)S(1)} collective-permute-done((f32[2,1,256]{2,0,1:T(2,128)S(1)}, f32[2,1,256]{2,0,1:T(2,128)S(1)}, u32[]{:S(2)}, u32[]{:S(2)}) %collective-permute-start.1) | collective-permute-done | bytes 2080 | tf_op jit(solution)/shard_map/ppermute | solution.py:16
  88.9 0.3 convolution_bitcast_fusion.6
  89.3 0.3 fusion.18
  89.6 0.3 fusion.17
  89.9 2.4 %collective-permute-done.2 = f32[2,1,256]{2,0,1:T(2,128)S(1)} collective-permute-done((f32[2,1,256]{2,0,1:T(2,128)S(1)}, f32[2,1,256]{2,0,1:T(2,128)S(1)}, u32[]{:S(2)}, u32[]{:S(2)}) %collective-permute-start.2) | collective-permute-done | bytes 2080 | tf_op jit(solution)/shard_map/ppermute | solution.py:16
  92.6 0.3 convolution_bitcast_fusion.2
  92.9 0.3 fusion.20
  93.2 0.3 fusion.19
  93.5 11.7 %all-reduce = f32[2,1,16]{2,1,0:T(1,128)S(1)} all-reduce(f32[2,1,16]{2,1,0:T(1,128)S(1)} %fusion.99), channel_id=3, replica_groups=mesh['pb'=4,'freq'=4,'ga'=2] {'pb'}, use_global_device_ids=true, to_apply=%region_3.4.clone | all-reduce | flops 32 | bytes 256
  105.3 0.6 pad_maximum_fusion.1
  (19 shorter events, 1.6 us)
Async XLA Ops:
  6.5 12.8 %copy-start = (f32[16,256]{1,0:T(8,128)S(1)}, f32[16,256]{1,0:T(8,128)}, u32[]{:S(2)}) copy-start(f32[16,256]{1,0:T(8,128)} %param.9) | copy-start | bytes 49156
  6.5 42.0 %all-gather.3.cloned.1.call-start = ((), (), s32[]{:S(2)}) async-start(), calls=%async_computation | async-start | bytes 4718592 | tf_op jit(solution)/shard_map/all_gather | solution.py:61
  81.8 3.1 %collective-permute-start = (f32[2,1,256]{2,0,1:T(2,128)S(1)}, f32[2,1,256]{2,0,1:T(2,128)S(1)}, u32[]{:S(2)}, u32[]{:S(2)}) collective-permute-start(f32[2,1,256]{2,0,1:T(2,128)S(1)} %fusion.103), channel_id=1, source_target_pairs={{6,0},{0,2},{2,4},{4,6},{7,1},{1,3},{3,5},{5,7},{14,8},{8,10},{10,... | collective-permute-start | bytes 6152 | tf_op jit(solution)/shard_map/ppermute | solution.py:16
  85.5 3.1 %collective-permute-start.1 = (f32[2,1,256]{2,0,1:T(2,128)S(1)}, f32[2,1,256]{2,0,1:T(2,128)S(1)}, u32[]{:S(2)}, u32[]{:S(2)}) collective-permute-start(f32[2,1,256]{2,0,1:T(2,128)S(1)} %collective-permute-done), channel_id=1, source_target_pairs={{6,0},{0,2},{2,4},{4,6},{7,1},{1,3},{3,5},{5,7},{14,8},{8,10},{10,... | collective-permute-start | bytes 6152 | tf_op jit(solution)/shard_map/ppermute | solution.py:16
  89.2 3.1 %collective-permute-start.2 = (f32[2,1,256]{2,0,1:T(2,128)S(1)}, f32[2,1,256]{2,0,1:T(2,128)S(1)}, u32[]{:S(2)}, u32[]{:S(2)}) collective-permute-start(f32[2,1,256]{2,0,1:T(2,128)S(1)} %collective-permute-done.1), channel_id=1, source_target_pairs={{6,0},{0,2},{2,4},{4,6},{7,1},{1,3},{3,5},{5,7},{14,8},{8,10},{10,... | collective-permute-start | bytes 6152 | tf_op jit(solution)/shard_map/ppermute | solution.py:16
Sparse Core Ops, SparseCore 0:
  9.2 39.2 all-gather.2
where the time goes:
time: 113 us
  waiting for transfers between devices  36.8 us (33%)
  matrix products  27.7 us (25%)
  between operations  18.7 us (17%)
  blocking collectives  16.6 us (15%)
  local copies, waits for them, and re-layouts  6.86 us (6%)
  other arithmetic  5.96 us (5%)
    all_gather x1, waiting for transfers between devices, body(): whole = lax.all_gather(local_block, ('freq', 'ga'), axis=1, tiled=True)  28.6 us
    dot_general x1, matrix products, panel_product(): lax.dot_general(density_all.reshape(2 * pair_rows, -1), screen.reshape(2...  22.8 us
    unnamed x1, blocking collectives  11.7 us
    ppermute x3, waiting for transfers between devices, from_behind(): return lax.ppermute(block, axis, route)  7.46 us
    psum x1, blocking collectives, body(): pair_total = lax.psum(jnp.stack([real_sum, imag_sum]), 'ga')  4.93 us
  transfers between devices with their start and end apart: 4, of which 4 were waited for; matrix products, arithmetic and copies ran while one was open for 8% of the time, Pallas kernels for 0%

commit v1 on v0

--- a/solution.py
+++ b/solution.py
@@ -58,7 +58,7 @@
     screen = screened[0, 0]
     panel_width = screen.shape[1]
     local_block = densities[0]
-    whole = lax.all_gather(local_block, ("freq", "ga"), axis=1, tiled=True)
+    whole = jnp.concatenate(lax.all_gather(local_block, ("freq", "ga")), axis=1)
     real_x, imag_x = panel_product(whole, screen)
     own_rows = lax.dynamic_slice_in_dim(whole, my_panel * panel_width, panel_width, 2)
     dense = own_rows.astype(jnp.float32)

time: 113 us -> 118 us (1.044)
  local copies, waits for them, and re-layouts: 6.86 us -> 9.51 us
  other arithmetic: 5.96 us -> 7.79 us
    reduce_sum x1, other arithmetic: 1.22 us -> 4.6 us  [body(): real_sum = jnp.sum(dense[0] * real_x + dense[1] * imag_x, axis=1)]
    reshape x0 -> x1, local copies, waits for them, and re-layouts: none -> 2.67 us  [body(): whole = jnp.concatenate(lax.all_gather(local_block, ('freq', 'ga')), axis=1)]
    convert_element_type x1, other arithmetic: 2.1 us -> 0.52 us  [body(): dense = own_rows.astype(jnp.float32)]
where the time goes in v1:
time: 118 us; the launch traced here: 117 us
  waiting for transfers between devices  36.8 us (31%)
  matrix products  27.8 us (24%)
  between operations  18.7 us (16%)
  blocking collectives  16.6 us (14%)
  local copies, waits for them, and re-layouts  9.51 us (8%)
  other arithmetic  7.79 us (7%)
    all_gather x1, waiting for transfers between devices, body(): whole = jnp.concatenate(lax.all_gather(local_block, ('freq', 'ga')), axis=1)  28.6 us
    dot_general x1, matrix products, panel_product(): lax.dot_general(density_all.reshape(2 * pair_rows, -1), screen.reshape(2...  23 us
    unnamed x1, blocking collectives  11.7 us
    ppermute x3, waiting for transfers between devices, from_behind(): return lax.ppermute(block, axis, route)  7.46 us
    psum x1, blocking collectives, body(): pair_total = lax.psum(jnp.stack([real_sum, imag_sum]), 'ga')  4.93 us
    reduce_sum x1, other arithmetic, body(): real_sum = jnp.sum(dense[0] * real_x + dense[1] * imag_x, axis=1)  4.6 us
    reshape x1, local copies, waits for them, and re-layouts, body(): whole = jnp.concatenate(lax.all_gather(local_block, ('freq', 'ga')), axis=1)  2.67 us
  transfers between devices with their start and end apart: 4, of which 4 were waited for; matrix products, arithmetic and copies ran while one was open for 8% of the time, Pallas kernels for 0%

profile of v1, /device:TPU:0, one launch (start us, length us, event | category | flops | bytes accessed | tf_op | source)
XLA Modules:
  0.0 117.4 jit_solution(7099264643580606152)
XLA Ops:
  6.5 0.7 all-gather.2.cloned.1.call-update
  7.3 1.2 %dynamic_slice.30 = s32[1]{0:T(128)} dynamic-slice(s32[4]{0:T(128)} %param.11, s32[]{:T(128)S(6)} %select_n.62), dynamic_slice_sizes={1} | dynamic-slice | bytes 12 | tf_op jit(solution)/shard_map/dynamic_slice | solution.py:69
  9.9 1.5 %fusion.101 = (s32[1]{0:T(128)}, s32[1]{0:T(128)}, s32[1]{0:T(128)}, s32[1]{0:T(128)}) fusion(s32[4]{0:T(128)} %param.12, s32[]{:T(128)S(6)} %select_n.70, s32[]{:T(128)S(6)} %select_n.66, s32[]{:T(128)S(6)} %select_n.61, s32[]{:T(128)S(6)} %select_n.68), kind=kLoop, calls=%fused_computation.142 | loop fusion | bytes 48 | tf_op jit(solution)/shard_map/dynamic_slice | solution.py:80
  14.2 1.3 %dynamic-slice = u32[1]{0:T(128)} dynamic-slice(u32[32]{0:T(128)} %constant.94, u32[]{:T(128)S(6)} %add.222), dynamic_slice_sizes={1} | dynamic-slice | bytes 12
  16.1 1.3 %dynamic_slice.28 = f32[1]{0:T(128)} dynamic-slice(f32[4]{0:T(128)} %param.13, s32[]{:T(128)S(6)} %select_n.59), dynamic_slice_sizes={1} | dynamic-slice | bytes 12 | tf_op jit(solution)/shard_map/dynamic_slice | solution.py:68
  18.0 1.2 %dynamic_slice.32 = s32[1]{0:T(128)} dynamic-slice(s32[16]{0:T(128)} %param.10, s32[]{:T(128)S(6)} %select_n.63), dynamic_slice_sizes={1} | dynamic-slice | bytes 12 | tf_op jit(solution)/shard_map/dynamic_slice | solution.py:71
  19.3 0.7 fusion.99
  20.0 28.6 %all-gather.2.cloned.1.call-done = bf16[8,2,32,4096]{3,2,1,0:T(8,128)(2,1)} async-done(((bf16[1,2,32,4096]{3,2,1,0:T(8,128)(2,1)}), bf16[8,2,32,4096]{3,2,1,0:T(8,128)(2,1)}) %all-gather.2.cloned.1.call-update) | async-done | bytes 4194320 | tf_op jit(solution)/shard_map/all_gather | solution.py:61
  48.6 2.7 %copy.9 = bf16[2,8,32,4096]{3,2,1,0:T(8,128)(2,1)S(1)} copy(bf16[2,8,32,4096]{3,2,0,1:T(8,128)(2,1)} %bitcast.187) | data formatting | bytes 8388608 | tf_op jit(solution)/shard_map/reshape | solution.py:61
  51.2 0.5 dynamic-slice_convert_fusion
  51.8 23.0 %fusion = f32[2,256,2,2048]{3,1,2,0:T(8,128)} fusion(bf16[2,256,4096,1]{2,1,3,0:T(8,128)(2,1)S(1)} %bitcast.186, bf16[1,1,2,2048,4096]{4,3,2,1,0:T(8,128)(2,1)} %param.8), kind=kOutput, calls=%fused_computation | convolution fusion | flops 17179869184 | bytes 46137344 | tf_op jit(solution)/shard_map/dot_general | solution.py:42
  74.7 4.6 %add_reduce_fusion = (f32[256]{0:T(256)S(1)}, f32[256]{0:T(256)S(1)}) fusion(f32[2,256,2048]{2,1,0:T(8,128)S(1)} %dynamic-slice_convert_fusion, f32[2,256,2,2048]{3,1,2,0:T(8,128)} %fusion), kind=kLoop, calls=%fused_computation.9 | loop fusion | flops 5242368 | bytes 12584960 | tf_op jit(solution)/shard_map/reduce_sum | solution.py:65
  79.4 4.9 %psum.7 = f32[2,256]{1,0:T(2,128)S(1)} all-reduce(f32[2,256]{1,0:T(2,128)S(1)} %pad_maximum_fusion), channel_id=1, replica_groups=mesh['pb'=4,'freq'=4,'ga'=2] {'ga'}, use_global_device_ids=true, to_apply=%region_2.0 | all-reduce | flops 512 | bytes 4096 | tf_op jit(solution)/shard_map/psum | solution.py:67
  84.3 0.6 broadcast_multiply_fusion
  84.9 0.6 fusion.103
  85.9 0.3 convolution_bitcast_fusion.13
  86.2 0.3 fusion.12
  86.6 0.3 fusion.13
  86.9 2.7 %collective-permute-done = f32[2,1,256]{2,0,1:T(2,128)S(1)} collective-permute-done((f32[2,1,256]{2,0,1:T(2,128)S(1)}, f32[2,1,256]{2,0,1:T(2,128)S(1)}, u32[]{:S(2)}, u32[]{:S(2)}) %collective-permute-start) | collective-permute-done | bytes 2080 | tf_op jit(solution)/shard_map/ppermute | solution.py:16
  89.9 0.3 convolution_bitcast_fusion.10
  90.3 0.3 fusion.15
  90.6 0.3 fusion.14
  90.9 2.4 %collective-permute-done.1 = f32[2,1,256]{2,0,1:T(2,128)S(1)} collective-permute-done((f32[2,1,256]{2,0,1:T(2,128)S(1)}, f32[2,1,256]{2,0,1:T(2,128)S(1)}, u32[]{:S(2)}, u32[]{:S(2)}) %collective-permute-start.1) | collective-permute-done | bytes 2080 | tf_op jit(solution)/shard_map/ppermute | solution.py:16
  93.5 0.3 convolution_bitcast_fusion.6
  93.9 0.3 fusion.17
  94.2 0.3 fusion.16
  94.5 2.4 %collective-permute-done.2 = f32[2,1,256]{2,0,1:T(2,128)S(1)} collective-permute-done((f32[2,1,256]{2,0,1:T(2,128)S(1)}, f32[2,1,256]{2,0,1:T(2,128)S(1)}, u32[]{:S(2)}, u32[]{:S(2)}) %collective-permute-start.2) | collective-permute-done | bytes 2080 | tf_op jit(solution)/shard_map/ppermute | solution.py:16
  97.2 0.3 convolution_bitcast_fusion.2
  97.5 0.3 fusion.19
  97.9 0.3 fusion.18
  98.2 11.7 %all-reduce = f32[2,1,16]{2,1,0:T(1,128)S(1)} all-reduce(f32[2,1,16]{2,1,0:T(1,128)S(1)} %fusion.98), channel_id=2, replica_groups=mesh['pb'=4,'freq'=4,'ga'=2] {'pb'}, use_global_device_ids=true, to_apply=%region_3.4.clone | all-reduce | flops 32 | bytes 256
  110.0 0.6 pad_maximum_fusion.1
  (20 shorter events, 1.8 us)
Async XLA Ops:
  6.5 12.8 %copy-start = (f32[16,256]{1,0:T(8,128)S(1)}, f32[16,256]{1,0:T(8,128)}, u32[]{:S(2)}) copy-start(f32[16,256]{1,0:T(8,128)} %param.9) | copy-start | bytes 49156
  6.5 42.0 %all-gather.2.cloned.1.call-start = ((), (), s32[]{:S(2)}) async-start(), calls=%async_computation | async-start | bytes 4718592 | tf_op jit(solution)/shard_map/all_gather | solution.py:61
  86.5 3.1 %collective-permute-start = (f32[2,1,256]{2,0,1:T(2,128)S(1)}, f32[2,1,256]{2,0,1:T(2,128)S(1)}, u32[]{:S(2)}, u32[]{:S(2)}) collective-permute-start(f32[2,1,256]{2,0,1:T(2,128)S(1)} %fusion.103), channel_id=1, source_target_pairs={{6,0},{0,2},{2,4},{4,6},{7,1},{1,3},{3,5},{5,7},{14,8},{8,10},{10,... | collective-permute-start | bytes 6152 | tf_op jit(solution)/shard_map/ppermute | solution.py:16
  90.2 3.1 %collective-permute-start.1 = (f32[2,1,256]{2,0,1:T(2,128)S(1)}, f32[2,1,256]{2,0,1:T(2,128)S(1)}, u32[]{:S(2)}, u32[]{:S(2)}) collective-permute-start(f32[2,1,256]{2,0,1:T(2,128)S(1)} %collective-permute-done), channel_id=1, source_target_pairs={{6,0},{0,2},{2,4},{4,6},{7,1},{1,3},{3,5},{5,7},{14,8},{8,10},{10,... | collective-permute-start | bytes 6152 | tf_op jit(solution)/shard_map/ppermute | solution.py:16
  93.9 3.1 %collective-permute-start.2 = (f32[2,1,256]{2,0,1:T(2,128)S(1)}, f32[2,1,256]{2,0,1:T(2,128)S(1)}, u32[]{:S(2)}, u32[]{:S(2)}) collective-permute-start(f32[2,1,256]{2,0,1:T(2,128)S(1)} %collective-permute-done.1), channel_id=1, source_target_pairs={{6,0},{0,2},{2,4},{4,6},{7,1},{1,3},{3,5},{5,7},{14,8},{8,10},{10,... | collective-permute-start | bytes 6152 | tf_op jit(solution)/shard_map/ppermute | solution.py:16
Sparse Core Ops, SparseCore 0:
  9.2 39.2 all-gather.1
